TPU v7x, 32 devices: a whole 2x2x4 slice. The times are simulated.
32 devices in a mesh: fsdp: 8 (over y, x, core), tensor: 4 (over z).
Axes of the slice: x: 2, y: 2, z: 4, core: 2. Of those that a mesh axis runs over, the one named last changes fastest.
Arguments:
- block_input: bfloat16 [8192, 2048], P(('fsdp', 'tensor')), may hold values from -6 to 6
- doc_ids: int32 [8, 1024], P('fsdp'), may hold values from 0 to 5, never falling along the last dimension, each value on 1 to 512 neighbouring positions
- w_query: bfloat16 [1, 2048, 2048], P(None, 'fsdp', 'tensor')
- w_keyval: bfloat16 [1, 2048, 8, 128], P(None, 'fsdp', 'tensor')
- w_attn_out: bfloat16 [1, 2048, 2048], P(None, 'tensor', 'fsdp'), may hold values from -0.5 to 0.5
- w_gate_up: bfloat16 [1, 2048, 2, 8192], P(None, 'fsdp', None, 'tensor'), may hold values from -0.125 to 0.125
- w_down: bfloat16 [1, 8192, 2048], P(None, 'tensor', 'fsdp'), may hold values from -0.0625 to 0.0625
- norm_gains: bfloat16 [1, 2, 2048], P(None, None, 'fsdp'), may hold values from 0.5 to 1.5
- out_cotangent: float32 [8192, 2048], P(('fsdp', 'tensor')), may hold values from -6 to 6
Outputs:
- block_output: float32 [8192, 2048], P(('fsdp', 'tensor'))
- grad_input: float32 [8192, 2048], P(('fsdp', 'tensor'))
- grad_w_query: float32 [1, 2048, 2048], P(None, 'fsdp', 'tensor')
- grad_w_keyval: float32 [1, 2048, 8, 128], P(None, 'fsdp', 'tensor')
- grad_w_attn_out: float32 [1, 2048, 2048], P(None, 'tensor', 'fsdp')
- grad_w_gate_up: float32 [1, 2048, 2, 8192], P(None, 'fsdp', None, 'tensor')
- grad_w_down: float32 [1, 8192, 2048], P(None, 'tensor', 'fsdp')
- grad_norm_gains: float32 [1, 2, 2048], P(None, None, 'fsdp')
Inputs may be any that keep to these rules, and one draw needn't show every extreme that they name: `doc_ids`: in each row document numbers never fall, every number of 0 to 5 appears, each document holds 1 to 512 tokens and one holds exactly 512.
All inputs are finite; a program needn't handle non-finite values.
Results may differ from a plain program's by a relative error of at most 0.014.
Values may be sent and summed in bfloat16 or wider, within the bound.
A program may use at most 320 MiB of HBM per device.

v0:
```python
import jax
import jax.numpy as jnp
from jax import lax
from jax.sharding import PartitionSpec as P

MAXLEN = 512
NORM_EPSILON = 1e-05
ROPE_BASE = 500000.0


def norm_apply(residual, gain):
    inverse = lax.rsqrt(jnp.mean(residual * residual, axis=-1, keepdims=True) + NORM_EPSILON)
    return (inverse, (residual * inverse * gain.astype(jnp.float32)).astype(jnp.bfloat16))


def norm_back(residual, inverse, gain, grad_normed):
    scaled = grad_normed * gain.astype(jnp.float32)
    grad_gain = jnp.sum(grad_normed * residual * inverse, axis=0)
    grad_residual = inverse * scaled - residual * inverse * inverse * inverse * jnp.mean(
        scaled * residual, axis=-1, keepdims=True
    )
    return (grad_residual, grad_gain)


def rope_tables(doc_row, head_size):
    places = jnp.arange(doc_row.shape[0], dtype=jnp.int32)
    doc_start = jnp.concatenate([jnp.array([True]), doc_row[1:] != doc_row[:-1]])
    starts = lax.cummax(jnp.where(doc_start, places, 0), axis=0)
    exponent = jnp.arange(head_size // 2, dtype=jnp.float32) * (-2.0 / head_size)
    angles = (places - starts).astype(jnp.float32)[:, None] * jnp.power(ROPE_BASE, exponent)[
        None, :
    ]
    return (jnp.cos(angles), jnp.sin(angles))


def rotate(vectors, cosine, sine_table, direction_sign):
    half_size = vectors.shape[-1] // 2
    table_shape = (vectors.shape[0],) + (1,) * (vectors.ndim - 2) + (half_size,)
    cos_part = cosine.reshape(table_shape)
    sin_part = direction_sign * sine_table.reshape(table_shape)
    first_half = vectors[..., :half_size]
    second = vectors[..., half_size:]
    return jnp.concatenate(
        [first_half * cos_part - second * sin_part, second * cos_part + first_half * sin_part],
        axis=-1,
    )


def block_mask(doc_row, block_start, block_rows, key_low, key_high):
    places = jnp.arange(doc_row.shape[0], dtype=jnp.int32)
    own_docs = doc_row[block_start : block_start + block_rows]
    own_places = places[block_start : block_start + block_rows]
    return (own_docs[:, None] == doc_row[None, key_low:key_high]) & (
        places[None, key_low:key_high] <= own_places[:, None]
    )


def attend_block(query_rows, key_rows, value_rows, allowed, score_scale):
    scores = (
        jnp.einsum("qkgd,skd->kgqs", query_rows, key_rows, preferred_element_type=jnp.float32)
        * score_scale
    )
    scores = jnp.where(allowed[None, None], scores, -jnp.inf)
    row_max = jnp.max(scores, axis=-1, keepdims=True)
    log_total = row_max + jnp.log(jnp.sum(jnp.exp(scores - row_max), axis=-1, keepdims=True))
    probabilities = jnp.exp(scores - log_total).astype(jnp.bfloat16)
    attn_out = jnp.einsum(
        "kgqs,skd->qkgd", probabilities, value_rows, preferred_element_type=jnp.float32
    )
    return (attn_out.astype(jnp.bfloat16), log_total)


def attend_back(
    query_rows, key_rows, value_rows, allowed, log_total, out_rows, grad_out, score_scale
):
    scores = (
        jnp.einsum("qkgd,skd->kgqs", query_rows, key_rows, preferred_element_type=jnp.float32)
        * score_scale
    )
    scores = jnp.where(allowed[None, None], scores, -jnp.inf)
    probabilities = jnp.exp(scores - log_total)
    row_delta = jnp.einsum("qkgd,qkgd->kgq", grad_out, out_rows, preferred_element_type=jnp.float32)
    grad_probs = jnp.einsum(
        "qkgd,skd->kgqs", grad_out, value_rows, preferred_element_type=jnp.float32
    )
    grad_scores = (probabilities * (grad_probs - row_delta[..., None]) * score_scale).astype(
        jnp.bfloat16
    )
    grad_query = jnp.einsum(
        "kgqs,skd->qkgd", grad_scores, key_rows, preferred_element_type=jnp.float32
    )
    grad_key = jnp.einsum(
        "kgqs,qkgd->skd", grad_scores, query_rows, preferred_element_type=jnp.float32
    )
    grad_value = jnp.einsum(
        "kgqs,qkgd->skd",
        probabilities.astype(jnp.bfloat16),
        grad_out,
        preferred_element_type=jnp.float32,
    )
    return (grad_query, grad_key, grad_value)


def per_device(
    block_input,
    doc_ids,
    w_query,
    w_keyval,
    w_attn_out,
    w_gate_up,
    w_down,
    norm_gains,
    out_cotangent,
):
    layers = w_query.shape[0]
    doc_row = doc_ids[0]
    row_count = doc_row.shape[0]
    local_rows = block_input.shape[0]
    kv_local = w_keyval.shape[2]
    head_size = w_keyval.shape[3] // 2
    group_size = w_query.shape[2] // (kv_local * head_size)
    block_rows = min(512, row_count)
    score_scale = head_size ** (-0.5)
    cosine, sine_table = rope_tables(doc_row, head_size)
    block_starts = list(range(0, row_count, block_rows))
    windows = [
        (max(0, block_start - MAXLEN), block_start + block_rows) for block_start in block_starts
    ]
    mask_list = [
        block_mask(
            doc_row, block_start, block_rows, windows[block_index][0], windows[block_index][1]
        )
        for block_index, block_start in enumerate(block_starts)
    ]

    def spread(rows_local):
        return lax.all_gather(rows_local, "tensor", axis=0, tiled=True)

    def collect(term_fn):
        return lax.psum_scatter(
            term_fn(jnp.int32(0), lax.axis_size("tensor") * local_rows).astype(jnp.bfloat16),
            "tensor",
            scatter_dimension=0,
            tiled=True,
        ).astype(jnp.float32)

    def spread_grad(rows_local):
        return lax.all_gather(rows_local, "tensor", axis=0, tiled=True)

    def collect_grad(term_fn):
        return lax.psum_scatter(
            term_fn(jnp.int32(0), lax.axis_size("tensor") * local_rows).astype(jnp.bfloat16),
            "tensor",
            scatter_dimension=0,
            tiled=True,
        ).astype(jnp.float32)

    residual = block_input.astype(jnp.float32)
    layer_index = 0
    weights = (
        lax.all_gather(w_query[layer_index], "fsdp", axis=0, tiled=True),
        lax.all_gather(w_keyval[layer_index], "fsdp", axis=0, tiled=True),
        lax.all_gather(w_attn_out[layer_index], "fsdp", axis=1, tiled=True),
        lax.all_gather(w_gate_up[layer_index], "fsdp", axis=0, tiled=True),
        lax.all_gather(w_down[layer_index], "fsdp", axis=1, tiled=True),
        lax.all_gather(norm_gains[layer_index], "fsdp", axis=1, tiled=True),
    )
    w_query_all, w_keyval_all, w_out_all, w_gate_all, w_down_all, gains_all = weights
    model_width = w_query_all.shape[0]
    inv_attn, normed = norm_apply(residual, gains_all[0])
    normed_all = spread(normed)
    query_full = jnp.dot(normed_all, w_query_all, preferred_element_type=jnp.float32).reshape(
        row_count, kv_local, group_size, head_size
    )
    keyval = jnp.dot(
        normed_all, w_keyval_all.reshape(model_width, -1), preferred_element_type=jnp.float32
    ).reshape(row_count, kv_local, 2 * head_size)
    query_rows = rotate(query_full, cosine, sine_table, 1.0).astype(jnp.bfloat16)
    key_rows = rotate(keyval[..., :head_size], cosine, sine_table, 1.0).astype(jnp.bfloat16)
    value_rows = keyval[..., head_size:].astype(jnp.bfloat16)
    out_list = []
    total_list = []
    for block_index, block_start in enumerate(block_starts):
        key_low, key_high = windows[block_index]
        out_block, log_total = attend_block(
            query_rows[block_start : block_start + block_rows],
            key_rows[key_low:key_high],
            value_rows[key_low:key_high],
            mask_list[block_index],
            score_scale,
        )
        out_list.append(out_block)
        total_list.append(log_total)
    attended = jnp.concatenate(out_list, axis=0).reshape(row_count, -1)

    def attn_term(row_start, row_size):
        return jnp.dot(attended, w_out_all, preferred_element_type=jnp.float32)

    middle = residual + collect(attn_term)
    inv_mlp, normed_mlp = norm_apply(middle, gains_all[1])
    normed_mlp_all = spread(normed_mlp)
    gate_up = jnp.dot(
        normed_mlp_all, w_gate_all.reshape(model_width, -1), preferred_element_type=jnp.float32
    ).reshape(row_count, 2, -1)
    gate_value = gate_up[:, 0]
    up_value = gate_up[:, 1]
    hidden = (jax.nn.silu(gate_value) * up_value).astype(jnp.bfloat16)

    def mlp_term(row_start, row_size):
        return jnp.dot(hidden, w_down_all, preferred_element_type=jnp.float32)

    new_rows = middle + collect(mlp_term)
    stored = [
        (
            residual,
            inv_attn,
            normed_all,
            query_rows,
            key_rows,
            value_rows,
            attended,
            total_list,
            middle,
            inv_mlp,
            normed_mlp_all,
            gate_value,
            up_value,
            hidden,
        )
    ]
    kept_weights = [weights]
    residual = new_rows
    output_rows = residual
    grad_rows = out_cotangent
    layer_grads = [None] * layers
    for layer_index in reversed(range(layers)):
        weights = kept_weights[layer_index]
        w_query_all, w_keyval_all, w_out_all, w_gate_all, w_down_all, gains_all = weights
        model_width = w_query_all.shape[0]
        (
            residual,
            inv_attn,
            normed_all,
            query_rows,
            key_rows,
            value_rows,
            attended,
            total_list,
            middle,
            inv_mlp,
            normed_mlp_all,
            gate_value,
            up_value,
            hidden,
        ) = stored[layer_index]
        grad_all = spread_grad(grad_rows.astype(jnp.bfloat16))
        grad_down = jnp.dot(hidden.T, grad_all, preferred_element_type=jnp.float32)
        grad_hidden = jnp.dot(grad_all, w_down_all.T, preferred_element_type=jnp.float32)
        sigmoid_gate = jax.nn.sigmoid(gate_value)
        grad_gate = (
            grad_hidden * up_value * sigmoid_gate * (1.0 + gate_value * (1.0 - sigmoid_gate))
        )
        grad_up = grad_hidden * jax.nn.silu(gate_value)
        grad_gate_up = (
            jnp.stack([grad_gate, grad_up], axis=1).astype(jnp.bfloat16).reshape(row_count, -1)
        )
        grad_wgu = jnp.dot(
            normed_mlp_all.T, grad_gate_up, preferred_element_type=jnp.float32
        ).reshape(w_gate_all.shape)

        def mlp_back(row_start, row_size):
            return jnp.dot(
                grad_gate_up,
                w_gate_all.reshape(model_width, -1).T,
                preferred_element_type=jnp.float32,
            )

        norm_part, grad_gain_mlp = norm_back(middle, inv_mlp, gains_all[1], collect_grad(mlp_back))
        grad_middle = grad_rows + norm_part
        middle_all = spread_grad(grad_middle.astype(jnp.bfloat16))
        grad_wo = jnp.dot(attended.T, middle_all, preferred_element_type=jnp.float32)
        grad_attended = (
            jnp.dot(middle_all, w_out_all.T, preferred_element_type=jnp.float32)
            .astype(jnp.bfloat16)
            .reshape(row_count, kv_local, group_size, head_size)
        )
        attended_heads = attended.reshape(row_count, kv_local, group_size, head_size)
        grad_keys = jnp.zeros((row_count, kv_local, head_size), jnp.float32)
        grad_values = jnp.zeros((row_count, kv_local, head_size), jnp.float32)
        query_grads = []
        for block_index, block_start in enumerate(block_starts):
            block_stop = block_start + block_rows
            key_low, key_high = windows[block_index]
            grad_query_block, grad_key_part, grad_value_part = attend_back(
                query_rows[block_start:block_stop],
                key_rows[key_low:key_high],
                value_rows[key_low:key_high],
                mask_list[block_index],
                total_list[block_index],
                attended_heads[block_start:block_stop],
                grad_attended[block_start:block_stop],
                score_scale,
            )
            query_grads.append(grad_query_block)
            pad_width = ((key_low, row_count - key_high), (0, 0), (0, 0))
            grad_keys = grad_keys + jnp.pad(grad_key_part, pad_width)
            grad_values = grad_values + jnp.pad(grad_value_part, pad_width)
        grad_query = (
            rotate(jnp.concatenate(query_grads, axis=0), cosine, sine_table, -1.0)
            .astype(jnp.bfloat16)
            .reshape(row_count, -1)
        )
        grad_keyval = (
            jnp.concatenate([rotate(grad_keys, cosine, sine_table, -1.0), grad_values], axis=-1)
            .astype(jnp.bfloat16)
            .reshape(row_count, -1)
        )
        grad_wq = jnp.dot(normed_all.T, grad_query, preferred_element_type=jnp.float32)
        grad_wkv = jnp.dot(normed_all.T, grad_keyval, preferred_element_type=jnp.float32).reshape(
            w_keyval_all.shape
        )

        def attn_back(row_start, row_size):
            return jnp.dot(grad_query, w_query_all.T, preferred_element_type=jnp.float32) + jnp.dot(
                grad_keyval,
                w_keyval_all.reshape(model_width, -1).T,
                preferred_element_type=jnp.float32,
            )

        norm_part, grad_gain_attn = norm_back(
            residual, inv_attn, gains_all[0], collect_grad(attn_back)
        )
        grad_rows = grad_middle + norm_part
        gain_total = lax.psum(jnp.stack([grad_gain_attn, grad_gain_mlp]), "tensor")
        local_set = (grad_wq, grad_wkv, grad_wo, grad_wgu, grad_down, gain_total)
        layer_grads[layer_index] = (
            lax.psum_scatter(
                local_set[0].astype(jnp.bfloat16), "fsdp", scatter_dimension=0, tiled=True
            ).astype(jnp.float32),
            lax.psum_scatter(
                local_set[1].astype(jnp.bfloat16), "fsdp", scatter_dimension=0, tiled=True
            ).astype(jnp.float32),
            lax.psum_scatter(
                local_set[2].astype(jnp.bfloat16), "fsdp", scatter_dimension=1, tiled=True
            ).astype(jnp.float32),
            lax.psum_scatter(
                local_set[3].astype(jnp.bfloat16), "fsdp", scatter_dimension=0, tiled=True
            ).astype(jnp.float32),
            lax.psum_scatter(
                local_set[4].astype(jnp.bfloat16), "fsdp", scatter_dimension=1, tiled=True
            ).astype(jnp.float32),
            lax.psum_scatter(local_set[5], "fsdp", scatter_dimension=1, tiled=True),
        )
    stacked = tuple((jnp.stack([layer_grads[0][member]]) for member in range(6)))
    return (
        output_rows,
        grad_rows,
        stacked[0],
        stacked[1],
        stacked[2],
        stacked[3],
        stacked[4],
        stacked[5],
    )


def solution(mesh):
    return jax.shard_map(
        per_device,
        mesh=mesh,
        in_specs=(
            P(("fsdp", "tensor"), None),
            P("fsdp", None),
            P(None, "fsdp", "tensor"),
            P(None, "fsdp", "tensor", None),
            P(None, "tensor", "fsdp"),
            P(None, "fsdp", None, "tensor"),
            P(None, "tensor", "fsdp"),
            P(None, None, "fsdp"),
            P(("fsdp", "tensor"), None),
        ),
        out_specs=(
            P(("fsdp", "tensor"), None),
            P(("fsdp", "tensor"), None),
            P(None, "fsdp", "tensor"),
            P(None, "fsdp", "tensor", None),
            P(None, "tensor", "fsdp"),
            P(None, "fsdp", None, "tensor"),
            P(None, "tensor", "fsdp"),
            P(None, None, "fsdp"),
        ),
        check_vma=False,
    )
```

profile of v0, /device:TPU:0, one launch (start us, length us, event | category | flops | bytes accessed | tf_op | source)
XLA Modules:
  0.0 1383.0 jit_solution(8392175093084249237)
XLA Ops:
  8.9 10.6 all-gather
  27.7 8.9 all-gather.24.cloned.1.call-done
  38.1 81.4 %all-gather.16.cloned.1.call-done = bf16[1024,2048]{1,0:T(8,128)(2,1)} async-done(((bf16[256,2048]{1,0:T(8,128)(2,1)}), bf16[1024,2048]{1,0:T(8,128)(2,1)}) %all-gather.16.cloned.1.call-update) | async-done | bytes 4194320 | tf_op jit(solution)/shard_map/all_gather | solution.py:137
  119.5 3.5 fusion.97
  123.1 24.6 %all-gather.26.cloned.1.call-done = bf16[1,2048,512]{2,1,0:T(8,128)(2,1)} async-done(((bf16[1,256,512]{2,1,0:T(8,128)(2,1)}), bf16[1,2048,512]{2,1,0:T(8,128)(2,1)}) %all-gather.26.cloned.1.call-update) | async-done | bytes 2097168 | tf_op jit(solution)/shard_map/all_gather | solution.py:161
  147.7 5.2 fusion.59
  153.3 7.6 fusion.8
  160.9 9.2 exponential_reduce_fusion
  175.9 6.5 convolution_convert_fusion.6
  182.5 4.3 convolution_convert_fusion.5
  187.9 6.0 convolution_convert_fusion.2
  197.8 73.2 %reduce-scatter.13.cloned.1.call-done = bf16[256,2048]{1,0:T(8,128)(2,1)} async-done(((bf16[1024,2048]{1,0:T(8,128)(2,1)}), bf16[256,2048]{1,0:T(8,128)(2,1)}) %reduce-scatter.13.cloned.1.call-update) | async-done | bytes 1048592 | tf_op jit(solution)/shard_map/reduce_scatter | solution.py:140
  277.2 86.4 %all-gather.30.cloned.1.call-done = bf16[1,2048,2,2048]{3,1,2,0:T(8,128)(2,1)} async-done(((bf16[1,256,2,2048]{3,1,2,0:T(8,128)(2,1)}), bf16[1,2048,2,2048]{3,1,2,0:T(8,128)(2,1)}) %all-gather.30.cloned.1.call-update) | async-done | bytes 16777232 | tf_op jit(solution)/shard_map/all_gather | solution.py:164
  363.6 22.6 %copy.56 = bf16[1,2048,2,2048]{1,3,2,0:T(8,128)(2,1)} copy(bf16[1,2048,2,2048]{3,1,2,0:T(8,128)(2,1)} %all-gather.30.cloned.1.call-done) | data formatting | bytes 33554432 | tf_op jit(solution)/shard_map/all_gather | solution.py:164
  386.2 60.3 %all-gather.18.cloned.1.call-done = bf16[1024,2048]{1,0:T(8,128)(2,1)} async-done(((bf16[256,2048]{1,0:T(8,128)(2,1)}), bf16[1024,2048]{1,0:T(8,128)(2,1)}) %all-gather.18.cloned.1.call-update) | async-done | bytes 4194320 | tf_op jit(solution)/shard_map/all_gather | solution.py:137
  446.5 23.7 %fusion = f32[1024,2,2048]{2,0,1:T(8,128)} fusion(bf16[1,2048,2,2048]{1,3,2,0:T(8,128)(2,1)} %copy.56, bf16[1024,2048]{1,0:T(8,128)(2,1)} %all-gather.18.cloned.1.call-done), kind=kOutput, calls=%fused_computation.1 | convolution fusion | flops 17179869184 | bytes 37748736 | tf_op jit(solution)/shard_map/dot_general | solution.py:202
  470.2 57.7 %all-gather.20.cloned.1.call-done = bf16[1024,2048]{1,0:T(8,128)(2,1)} async-done(((bf16[256,2048]{1,0:T(8,128)(2,1)}), bf16[1024,2048]{1,0:T(8,128)(2,1)}) %all-gather.20.cloned.1.call-update) | async-done | bytes 4194320 | tf_op jit(solution)/shard_map/all_gather | solution.py:148
  527.9 56.3 %all-gather.32.cloned.1.call-done = bf16[1,2048,2048]{2,1,0:T(8,128)(2,1)} async-done(((bf16[1,2048,256]{2,1,0:T(8,128)(2,1)}), bf16[1,2048,2048]{2,1,0:T(8,128)(2,1)}) %all-gather.32.cloned.1.call-update) | async-done | bytes 8388624 | tf_op jit(solution)/shard_map/all_gather | solution.py:165
  584.1 20.5 %multiply_bitcast_fusion.1 = (bf16[1024,1,2048]{2,0,1:T(8,128)(2,1)}, bf16[1024,1,2048]{2,0,1:T(8,128)(2,1)}) fusion(f32[1024,2,2048]{2,0,1:T(8,128)} %fusion, bf16[1024,2048]{1,0:T(8,128)(2,1)} %all-gather.20.cloned.1.call-done, bf16[1,2048,2048]{2,1,0:T(8,128)(2,1)} %all-gather.32.cloned.1.call-done), kind=kOutput, calls=%fused_computation.31 | convolution fusion | flops 8617197568 | bytes 37748736 | tf_op jit(solution)/shard_map/dot_general | solution.py:258
  604.6 24.2 %bitcast_convert_fusion = bf16[1024,2048]{1,0:T(8,128)(2,1)} fusion(bf16[1,2048,2,2048]{3,1,2,0:T(8,128)(2,1)} %all-gather.30.cloned.1.call-done, bf16[1024,1,2048]{2,0,1:T(8,128)(2,1)} %get-tuple-element.41, bf16[1024,1,2048]{2,0,1:T(8,128)(2,1)} %get-tuple-element.40), kind=kOutput, calls=%fused_computation.24 | convolution fusion | flops 17186160640 | bytes 29360128 | tf_op jit(solution)/shard_map/dot_general | solution.py:272
  628.9 76.9 %reduce-scatter.17.cloned.1.call-done = bf16[256,2048]{1,0:T(8,128)(2,1)} async-done(((bf16[1024,2048]{1,0:T(8,128)(2,1)}), bf16[256,2048]{1,0:T(8,128)(2,1)}) %reduce-scatter.17.cloned.1.call-update) | async-done | bytes 1048592 | tf_op jit(solution)/shard_map/reduce_scatter | solution.py:151
  711.3 81.3 %all-gather.22.cloned.1.call-done = bf16[1024,2048]{1,0:T(8,128)(2,1)} async-done(((bf16[256,2048]{1,0:T(8,128)(2,1)}), bf16[1024,2048]{1,0:T(8,128)(2,1)}) %all-gather.22.cloned.1.call-update) | async-done | bytes 4194320 | tf_op jit(solution)/shard_map/all_gather | solution.py:148
  792.6 5.2 fusion.62
  799.6 6.3 convolution_bitcast_fusion.4
  806.0 5.5 fusion.13
  815.4 9.3 fusion.4
  824.7 6.2 convolution_bitcast_fusion.1
  830.9 3.4 fusion.65
  834.4 6.5 fusion.66
  850.6 8.0 multiply_convert_fusion
  860.6 11.5 convolution_convert_fusion.1
  872.2 4.6 fusion.32
  877.3 5.8 convolution_convert_fusion.3
  883.2 6.0 convolution_convert_fusion.4
  889.3 13.9 %fusion.29 = bf16[1024,2048]{1,0:T(8,128)(2,1)} fusion(bf16[1024,2048]{1,0:T(8,128)(2,1)} %copy-done.14, bf16[1,2048,2048]{2,1,0:T(8,128)(2,1)} %all-gather.32.cloned.1.call-done), kind=kOutput, calls=%fused_computation.51 | convolution fusion | flops 8592031744 | bytes 16777216 | tf_op jit(solution)/shard_map/dot_general | solution.py:210
  903.2 7.5 maximum_convert_fusion
  910.8 11.9 copy.65
  929.5 24.7 %convolution_convert_fusion = bf16[2048,2,2048]{2,0,1:T(8,128)(2,1)} fusion(bf16[1024,2,2048]{0,2,1:T(8,128)(2,1)} %copy.65, bf16[1024,2048]{1,0:T(8,128)(2,1)} %all-gather.18.cloned.1.call-done), kind=kOutput, calls=%fused_computation.14 | convolution fusion | flops 17188257792 | bytes 29360128 | tf_op jit(solution)/shard_map/dot_general | solution.py:267
  954.3 47.0 %reduce-scatter.29.cloned.1.call-done = bf16[2048,256]{1,0:T(8,128)(2,1)} async-done(((bf16[2048,2048]{1,0:T(8,128)(2,1)}), bf16[2048,256]{1,0:T(8,128)(2,1)}) %reduce-scatter.29.cloned.1.call-update) | async-done | bytes 1048592 | tf_op jit(solution)/shard_map/reduce_scatter | solution.py:349
  1004.0 36.3 %reduce-scatter.23.cloned.1.call-done = bf16[256,2,128]{2,0,1:T(8,128)(2,1)} async-done(((bf16[2048,2,128]{2,0,1:T(8,128)(2,1)}), bf16[256,2,128]{2,0,1:T(8,128)(2,1)}) %reduce-scatter.23.cloned.1.call-update) | async-done | bytes 131088 | tf_op jit(solution)/shard_map/reduce_scatter | solution.py:340
  1042.1 43.0 %reduce-scatter.25.cloned.1.call-done = bf16[512,256]{1,0:T(8,128)(2,1)} async-done(((bf16[512,2048]{1,0:T(8,128)(2,1)}), bf16[512,256]{1,0:T(8,128)(2,1)}) %reduce-scatter.25.cloned.1.call-update) | async-done | bytes 262160 | tf_op jit(solution)/shard_map/reduce_scatter | solution.py:343
  1086.9 43.1 %reduce-scatter.21.cloned.1.call-done = bf16[256,512]{1,0:T(8,128)(2,1)} async-done(((bf16[2048,512]{1,0:T(8,128)(2,1)}), bf16[256,512]{1,0:T(8,128)(2,1)}) %reduce-scatter.21.cloned.1.call-update) | async-done | bytes 262160 | tf_op jit(solution)/shard_map/reduce_scatter | solution.py:337
  1131.8 77.1 %reduce-scatter.15.cloned.1.call-done = bf16[256,2048]{1,0:T(8,128)(2,1)} async-done(((bf16[1024,2048]{1,0:T(8,128)(2,1)}), bf16[256,2048]{1,0:T(8,128)(2,1)}) %reduce-scatter.15.cloned.1.call-update) | async-done | bytes 1048592 | tf_op jit(solution)/shard_map/reduce_scatter | solution.py:140
  1209.0 6.0 fusion.44
  1215.0 34.1 %reduce-scatter.31.cloned.1.call-done = f32[256,2]{1,0:T(8,128)} async-done(((f32[2048,2]{1,0:T(8,128)}), f32[256,2]{1,0:T(8,128)}) %reduce-scatter.31.cloned.1.call-update) | async-done | bytes 2064
  1250.0 12.5 psum.8
  1262.5 106.4 %reduce-scatter.27.cloned.1.call-done = bf16[256,2,2048]{2,0,1:T(8,128)(2,1)} async-done(((bf16[2048,2,2048]{2,0,1:T(8,128)(2,1)}), bf16[256,2,2048]{2,0,1:T(8,128)(2,1)}) %reduce-scatter.27.cloned.1.call-update) | async-done | bytes 2097168 | tf_op jit(solution)/shard_map/reduce_scatter | solution.py:346
  1371.0 5.3 copy.68
  (212 shorter events, 70.1 us)
Async XLA Ops:
  7.2 17.8 %copy-start.36 = (s32[1,1024]{1,0:T(1,128)S(1)}, s32[1,1024]{1,0:T(1,128)}, u32[]{:S(2)}) copy-start(s32[1,1024]{1,0:T(1,128)} %param.11) | copy-start | bytes 12292
  7.2 29.4 %all-gather.24.cloned.1.call-start = ((), (), s32[]{:S(2)}) async-start(), calls=%async_computation.23 | async-start | bytes 1179648 | tf_op jit(solution)/shard_map/all_gather | solution.py:162
  8.8 110.7 %all-gather.16.cloned.1.call-start = ((), (), s32[]{:S(2)}) async-start(), calls=%async_computation.10 | async-start | bytes 5242880 | tf_op jit(solution)/shard_map/all_gather | solution.py:137
  21.0 686.9 %copy-start.32 = (f32[1,1,2048]{2,1,0:T(1,128)}, f32[1,1,2048]{2,1,0:T(1,128)S(1)}, u32[]{:S(2)}) copy-start(f32[1,1,2048]{2,1,0:T(1,128)S(1)} %get-tuple-element.54) | copy-start | bytes 24580
  23.6 124.1 %all-gather.26.cloned.1.call-start = ((), (), s32[]{:S(2)}) async-start(), calls=%async_computation.24 | async-start | bytes 2359296 | tf_op jit(solution)/shard_map/all_gather | solution.py:161
  24.3 162.7 %all-gather.28.cloned.1.call-start = ((), (), s32[]{:S(2)}) async-start(), calls=%async_computation.25 | async-start | bytes 2359296 | tf_op jit(solution)/shard_map/all_gather | solution.py:163
  24.9 246.1 %reduce-scatter.13.cloned.1.call-start = ((), (), s32[]{:S(2)}) async-start(), calls=%async_computation.11 | async-start | bytes 5242880 | tf_op jit(solution)/shard_map/reduce_scatter | solution.py:140
  26.9 126.0 %copy-start.16 = (f32[1024,32]{0,1:T(8,128)}, f32[1024,32]{0,1:T(8,128)S(1)}, u32[]{:S(2)}) copy-start(f32[1024,32]{0,1:T(8,128)S(1)} %get-tuple-element.58) | copy-start | bytes 393220
  27.2 148.7 %copy-start.26 = (pred[512,512]{0,1:T(8,128)(4,1)}, pred[512,512]{0,1:T(8,128)(4,1)S(1)}, u32[]{:S(2)}) copy-start(pred[512,512]{0,1:T(8,128)(4,1)S(1)} %compare_and_fusion) | copy-start | bytes 786436
  27.7 154.7 %copy-start.12 = (pred[512,1024]{0,1:T(8,128)(4,1)}, pred[512,1024]{0,1:T(8,128)(4,1)S(1)}, u32[]{:S(2)}) copy-start(pred[512,1024]{0,1:T(8,128)(4,1)S(1)} %fusion.61) | copy-start | bytes 1572868
  123.0 59.5 %copy-start.48 = (bf16[1024,2,128]{0,2,1:T(8,128)(2,1)}, bf16[1024,2,128]{0,2,1:T(8,128)(2,1)S(1)}, u32[]{:S(2)}) copy-start(bf16[1024,2,128]{0,2,1:T(8,128)(2,1)S(1)} %get-tuple-element.61) | copy-start | bytes 1572868
  123.1 47.0 %copy-start.17 = (bf16[1024,2,32]{0,2,1:T(8,128)(2,1)}, bf16[1024,2,32]{0,2,1:T(8,128)(2,1)S(1)}, u32[]{:S(2)}) copy-start(bf16[1024,2,32]{0,2,1:T(8,128)(2,1)S(1)} %get-tuple-element.48) | copy-start | bytes 393220
  123.1 47.0 %copy-start.19 = (bf16[1024,2,32]{0,2,1:T(8,128)(2,1)}, bf16[1024,2,32]{0,2,1:T(8,128)(2,1)S(1)}, u32[]{:S(2)}) copy-start(bf16[1024,2,32]{0,2,1:T(8,128)(2,1)S(1)} %get-tuple-element.49) | copy-start | bytes 393220
  153.3 16.8 %copy-start.8 = (bf16[1024,2,4,32]{0,3,2,1:T(8,128)(2,1)}, bf16[1024,2,4,32]{0,3,2,1:T(8,128)(2,1)S(1)}, u32[]{:S(2)}) copy-start(bf16[1024,2,4,32]{0,3,2,1:T(8,128)(2,1)S(1)} %get-tuple-element.44) | copy-start | bytes 1572868
  153.3 16.8 %copy-start.10 = (bf16[1024,2,4,32]{0,3,2,1:T(8,128)(2,1)}, bf16[1024,2,4,32]{0,3,2,1:T(8,128)(2,1)S(1)}, u32[]{:S(2)}) copy-start(bf16[1024,2,4,32]{0,3,2,1:T(8,128)(2,1)S(1)} %get-tuple-element.45) | copy-start | bytes 1572868
  170.1 12.3 copy-start.39
  193.9 77.0 %copy-start = (bf16[256,2048]{1,0:T(8,128)(2,1)S(1)}, bf16[256,2048]{1,0:T(8,128)(2,1)}, u32[]{:S(2)}) copy-start(bf16[256,2048]{1,0:T(8,128)(2,1)} %param.10) | copy-start | bytes 3145732
  194.0 169.6 %all-gather.30.cloned.1.call-start = ((), (), s32[]{:S(2)}) async-start(), calls=%async_computation.26 | async-start | bytes 18874368 | tf_op jit(solution)/shard_map/all_gather | solution.py:164
  197.7 77.6 %copy-start.4 = (f32[256,2048]{1,0:T(8,128)S(1)}, f32[256,2048]{1,0:T(8,128)}, u32[]{:S(2)}) copy-start(f32[256,2048]{1,0:T(8,128)} %param.18) | copy-start | bytes 6291460
  197.7 248.7 %all-gather.18.cloned.1.call-start = ((), (), s32[]{:S(2)}) async-start(), calls=%async_computation.12 | async-start | bytes 5242880 | tf_op jit(solution)/shard_map/all_gather | solution.py:137
  272.6 435.3 %copy-start.37 = (f32[256]{0:T(256)}, f32[256]{0:T(256)S(1)}, u32[]{:S(2)}) copy-start(f32[256]{0:T(256)S(1)} %add_rsqrt_fusion) | copy-start | bytes 3076
  275.2 252.7 %all-gather.20.cloned.1.call-start = ((), (), s32[]{:S(2)}) async-start(), calls=%async_computation.14 | async-start | bytes 5242880 | tf_op jit(solution)/shard_map/all_gather | solution.py:148
  276.4 307.7 %all-gather.32.cloned.1.call-start = ((), (), s32[]{:S(2)}) async-start(), calls=%async_computation.27 | async-start | bytes 9437184 | tf_op jit(solution)/shard_map/all_gather | solution.py:165
  277.2 428.6 %reduce-scatter.17.cloned.1.call-start = ((), (), s32[]{:S(2)}) async-start(), calls=%async_computation.15 | async-start | bytes 5242880 | tf_op jit(solution)/shard_map/reduce_scatter | solution.py:151
  628.9 77.0 %copy-start.2 = (bf16[256,2048]{1,0:T(8,128)(2,1)S(1)}, bf16[256,2048]{1,0:T(8,128)(2,1)}, u32[]{:S(2)}) copy-start(bf16[256,2048]{1,0:T(8,128)(2,1)} %reduce-scatter.13.cloned.1.call-done) | copy-start | bytes 3145732
  628.9 163.7 %all-gather.22.cloned.1.call-start = ((), (), s32[]{:S(2)}) async-start(), calls=%async_computation.16 | async-start | bytes 5242880 | tf_op jit(solution)/shard_map/all_gather | solution.py:148
  707.9 89.9 %copy-start.44 = (f32[256]{0:T(256)}, f32[256]{0:T(256)S(1)}, u32[]{:S(2)}) copy-start(f32[256]{0:T(256)S(1)} %broadcast_multiply_fusion.2) | copy-start | bytes 3076
  711.2 86.7 %copy-start.23 = (bf16[2,64,4,512]{3,1,2,0:T(8,128)(2,1)S(1)}, bf16[2,64,4,512]{3,1,2,0:T(8,128)(2,1)}, u32[]{:S(2)}) copy-start(bf16[2,64,4,512]{3,1,2,0:T(8,128)(2,1)} %copy-done.22) | copy-start | bytes 1572868
  711.2 86.7 %copy-start.25 = (bf16[2,64,4,512]{3,1,2,0:T(8,128)(2,1)S(1)}, bf16[2,64,4,512]{3,1,2,0:T(8,128)(2,1)}, u32[]{:S(2)}) copy-start(bf16[2,64,4,512]{3,1,2,0:T(8,128)(2,1)} %copy-done.24) | copy-start | bytes 1572868
  711.2 88.4 %copy-start.27 = (pred[512,512]{0,1:T(8,128)(4,1)S(1)}, pred[512,512]{0,1:T(8,128)(4,1)}, u32[]{:S(2)}) copy-start(pred[512,512]{0,1:T(8,128)(4,1)} %copy-done.26) | copy-start | bytes 786436
  711.2 88.4 %copy-start.41 = (f32[1,8,512]{2,1,0:T(8,128)S(1)}, f32[1,8,512]{2,1,0:T(8,128)}, u32[]{:S(2)}) copy-start(f32[1,8,512]{2,1,0:T(8,128)} %copy-done.40) | copy-start | bytes 49156
  711.2 214.7 %reduce-scatter.19.cloned.1.call-start = ((), (), s32[]{:S(2)}) async-start(), calls=%async_computation.17 | async-start | bytes 5242880 | tf_op jit(solution)/shard_map/reduce_scatter | solution.py:151
  799.6 15.8 %slice-start.4 = ((s8[16777216]{0:T(1024)(128)(4,1)}), s8[4194304]{0:T(1024)(128)(4,1)S(1)}, s32[]{:S(2)}) async-start(s8[16777216]{0:T(1024)(128)(4,1)} %bitcast.277), calls=%async_computation.33 | async-start | bytes 8388608
  799.6 15.8 %slice-start.5 = ((s8[16777216]{0:T(1024)(128)(4,1)}), s8[4194304]{0:T(1024)(128)(4,1)S(1)}, s32[]{:S(2)}) async-start(s8[16777216]{0:T(1024)(128)(4,1)} %bitcast.277), calls=%async_computation.34 | async-start | bytes 8388608
  850.6 150.7 %reduce-scatter.29.cloned.1.call-start = ((), (), s32[]{:S(2)}) async-start(), calls=%async_computation.22 | async-start | bytes 9437184 | tf_op jit(solution)/shard_map/reduce_scatter | solution.py:349
  872.1 168.2 %reduce-scatter.23.cloned.1.call-start = ((), (), s32[]{:S(2)}) async-start(), calls=%async_computation.19 | async-start | bytes 1179648 | tf_op jit(solution)/shard_map/reduce_scatter | solution.py:340
  876.8 208.3 %reduce-scatter.25.cloned.1.call-start = ((), (), s32[]{:S(2)}) async-start(), calls=%async_computation.20 | async-start | bytes 2359296 | tf_op jit(solution)/shard_map/reduce_scatter | solution.py:343
  883.2 246.9 %reduce-scatter.21.cloned.1.call-start = ((), (), s32[]{:S(2)}) async-start(), calls=%async_computation.18 | async-start | bytes 2359296 | tf_op jit(solution)/shard_map/reduce_scatter | solution.py:337
  889.2 319.7 %reduce-scatter.15.cloned.1.call-start = ((), (), s32[]{:S(2)}) async-start(), calls=%async_computation.13 | async-start | bytes 5242880 | tf_op jit(solution)/shard_map/reduce_scatter | solution.py:140
  903.2 345.9 %reduce-scatter.31.cloned.1.call-start = ((), (), s32[]{:S(2)}) async-start(), calls=%async_computation.28 | async-start | bytes 1179648
  910.8 15.2 %copy-start.35 = (f32[1,1,2048]{2,1,0:T(1,128)S(1)}, f32[1,1,2048]{2,1,0:T(1,128)}, u32[]{:S(2)}) copy-start(f32[1,1,2048]{2,1,0:T(1,128)} %copy-done.34) | copy-start | bytes 24580
  910.8 15.2 %copy-start.43 = (f32[256]{0:T(256)S(1)}, f32[256]{0:T(256)}, u32[]{:S(2)}) copy-start(f32[256]{0:T(256)} %copy-done.42) | copy-start | bytes 3076
  929.3 439.6 %reduce-scatter.27.cloned.1.call-start = ((), (), s32[]{:S(2)}) async-start(), calls=%async_computation.21 | async-start | bytes 18874368 | tf_op jit(solution)/shard_map/reduce_scatter | solution.py:346
  954.2 254.7 %copy-start.3 = (bf16[256,2048]{1,0:T(8,128)(2,1)S(1)}, bf16[256,2048]{1,0:T(8,128)(2,1)}, u32[]{:S(2)}) copy-start(bf16[256,2048]{1,0:T(8,128)(2,1)} %reduce-scatter.13.cloned.1.call-done) | copy-start | bytes 3145732
  954.2 254.7 %copy-start.6 = (bf16[256,2048]{1,0:T(8,128)(2,1)S(1)}, bf16[256,2048]{1,0:T(8,128)(2,1)}, u32[]{:S(2)}) copy-start(bf16[256,2048]{1,0:T(8,128)(2,1)} %reduce-scatter.17.cloned.1.call-done) | copy-start | bytes 3145732
  954.2 254.7 %copy-start.33 = (f32[1,1,2048]{2,1,0:T(1,128)S(1)}, f32[1,1,2048]{2,1,0:T(1,128)}, u32[]{:S(2)}) copy-start(f32[1,1,2048]{2,1,0:T(1,128)} %copy-done.32) | copy-start | bytes 24580
  954.2 254.7 %copy-start.38 = (f32[256]{0:T(256)S(1)}, f32[256]{0:T(256)}, u32[]{:S(2)}) copy-start(f32[256]{0:T(256)} %copy-done.37) | copy-start | bytes 3076
  954.3 254.7 %copy-start.45 = (f32[256]{0:T(256)S(1)}, f32[256]{0:T(256)}, u32[]{:S(2)}) copy-start(f32[256]{0:T(256)} %copy-done.44) | copy-start | bytes 3076
  (28 other events, 153.2 us)
Sparse Core Ops, SparseCore 0:
  10.5 26.0 all-gather.23
  38.7 80.7 all-gather.15
  121.4 26.2 all-gather.25
  149.4 28.0 all-gather.27
  194.1 76.8 reduce-scatter.12
  273.3 90.2 all-gather.29
  365.7 80.7 all-gather.17
  448.6 79.2 all-gather.19
  529.8 54.3 all-gather.31
  629.0 76.7 reduce-scatter.16
  711.3 81.2 all-gather.21
  850.7 75.2 reduce-scatter.18
  929.4 71.7 reduce-scatter.28
  1004.3 35.9 reduce-scatter.22
  1044.0 41.1 reduce-scatter.24
  1088.9 41.1 reduce-scatter.20
  1132.2 76.7 reduce-scatter.14
  1212.6 36.4 reduce-scatter.30
  1252.6 116.1 reduce-scatter.26
where the time goes:
time: 1390 us; the launch traced here: 1380 us
  waiting for transfers between devices  999 us (72%)
  matrix products  221 us (16%)
  other arithmetic  67 us (5%)
  local copies, waits for them, and re-layouts  55.7 us (4%)
  blocking collectives  23 us (2%)
  between operations  15.1 us (1%)
    reduce_scatter x2, waiting for transfers between devices, collect(): lax.psum_scatter(term_fn(jnp.int32(0), lax.axis_size('tensor') * local_ro...  150 us
    all_gather x2, waiting for transfers between devices, spread(): return lax.all_gather(rows_local, 'tensor', axis=0, tiled=True)  142 us
    all_gather x2, waiting for transfers between devices, spread_grad(): return lax.all_gather(rows_local, 'tensor', axis=0, tiled=True)  139 us
    reduce_scatter x1, waiting for transfers between devices, per_device(): lax.psum_scatter(local_set[3].astype(jnp.bfloat16), 'fsdp', scatter_dimen...  106 us
    all_gather x1, waiting for transfers between devices, per_device(): lax.all_gather(w_gate_up[layer_index], 'fsdp', axis=0, tiled=True)  86.4 us
    reduce_scatter x2, waiting for transfers between devices, collect_grad(): lax.psum_scatter(term_fn(jnp.int32(0), lax.axis_size('tensor') * local_ro...  80.2 us
    all_gather x1, waiting for transfers between devices, per_device(): lax.all_gather(w_down[layer_index], 'fsdp', axis=1, tiled=True)  56.3 us
    reduce_scatter x1, waiting for transfers between devices, per_device(): lax.psum_scatter(local_set[4].astype(jnp.bfloat16), 'fsdp', scatter_dimen...  47 us
  transfers between devices with their start and end apart: 19, of which 18 were waited for; matrix products, arithmetic and copies ran while one was open for 15% of the time, Pallas kernels for 0%

commit v1 on v0

--- a/solution.py
+++ b/solution.py
@@ -134,7 +134,22 @@
     ]
 
     def spread(rows_local):
-        return lax.all_gather(rows_local, "tensor", axis=0, tiled=True)
+
+        def _switch_positions(body):
+            side_arr = lax.axis_size("tensor")
+            newest, shaped = (side_arr, lax.axis_index("tensor"))
+            formed, built = (body, 1)
+            while built < newest:
+                x_now = lax.ppermute(
+                    formed, "tensor", [(tick, tick ^ built) for tick in range(newest)]
+                )
+                w1 = jnp.concatenate([formed, x_now], axis=0)
+                all_values = jnp.concatenate([x_now, formed], axis=0)
+                formed = jnp.where(shaped & built == 0, w1, all_values)
+                built = 2 * built
+            return formed
+
+        return _switch_positions(rows_local)
 
     def collect(term_fn):
         return lax.psum_scatter(

time: 1390 us -> 1330 us (0.957)
  waiting for transfers between devices: 999 us -> 920 us
    ppermute x0 -> x4, waiting for transfers between devices: none -> 184 us  [_switch_positions(): lax.ppermute(formed, 'tensor', [(tick, tick ^ built) for tick in range(ne...]
    all_gather x2 -> x0, waiting for transfers between devices: 142 us -> none  [spread(): return lax.all_gather(rows_local, 'tensor', axis=0, tiled=True)]
    all_gather x2, waiting for transfers between devices: 139 us -> 81.3 us  [spread_grad(): return lax.all_gather(rows_local, 'tensor', axis=0, tiled=True)]
    all_gather x1, waiting for transfers between devices: 86.4 us -> 60.3 us  [per_device(): lax.all_gather(w_gate_up[layer_index], 'fsdp', axis=0, tiled=True)]
    all_gather x1, waiting for transfers between devices: 24.6 us -> 0.02 us  [per_device(): lax.all_gather(w_query[layer_index], 'fsdp', axis=0, tiled=True)]
    unnamed x20 -> x18, waiting for transfers between devices: 36.3 us -> 35.7 us
  transfers between devices with their start and end apart: 19 -> 21, of which waited for: 18 -> 16; matrix products, arithmetic and copies ran while one was open for 15% -> 17% of each run, Pallas kernels for 0% -> 0%
where the time goes in v1:
time: 1330 us; the launch traced here: 1320 us
  waiting for transfers between devices  920 us (69%)
  matrix products  228 us (17%)
  other arithmetic  68.6 us (5%)
  local copies, waits for them, and re-layouts  55.6 us (4%)
  blocking collectives  22.8 us (2%)
  between operations  15 us (1%)
    ppermute x4, waiting for transfers between devices, _switch_positions(): lax.ppermute(formed, 'tensor', [(tick, tick ^ built) for tick in range(ne...  184 us
    reduce_scatter x2, waiting for transfers between devices, collect(): lax.psum_scatter(term_fn(jnp.int32(0), lax.axis_size('tensor') * local_ro...  148 us
    reduce_scatter x1, waiting for transfers between devices, per_device(): lax.psum_scatter(local_set[3].astype(jnp.bfloat16), 'fsdp', scatter_dimen...  106 us
    all_gather x2, waiting for transfers between devices, spread_grad(): return lax.all_gather(rows_local, 'tensor', axis=0, tiled=True)  81.3 us
    reduce_scatter x2, waiting for transfers between devices, collect_grad(): lax.psum_scatter(term_fn(jnp.int32(0), lax.axis_size('tensor') * local_ro...  76.9 us
    all_gather x1, waiting for transfers between devices, per_device(): lax.all_gather(w_gate_up[layer_index], 'fsdp', axis=0, tiled=True)  60.3 us
    all_gather x1, waiting for transfers between devices, per_device(): lax.all_gather(w_down[layer_index], 'fsdp', axis=1, tiled=True)  57.1 us
    reduce_scatter x1, waiting for transfers between devices, per_device(): lax.psum_scatter(local_set[4].astype(jnp.bfloat16), 'fsdp', scatter_dimen...  47.3 us
  transfers between devices with their start and end apart: 21, of which 16 were waited for; matrix products, arithmetic and copies ran while one was open for 17% of the time, Pallas kernels for 0%

profile of v1, /device:TPU:0, one launch (start us, length us, event | category | flops | bytes accessed | tf_op | source)
XLA Modules:
  0.0 1320.9 jit_solution(15715131205385203739)
XLA Ops:
  9.6 10.6 all-gather
  25.5 23.8 %collective-permute-done = bf16[256,2048]{1,0:T(8,128)(2,1)S(1)} collective-permute-done((bf16[256,2048]{1,0:T(8,128)(2,1)S(1)}, bf16[256,2048]{1,0:T(8,128)(2,1)S(1)}, u32[]{:S(2)}, u32[]{:S(2)}) %collective-permute-start) | collective-permute-done | bytes 1048608 | tf_op jit(solution)/shard_map/ppermute | solution.py:143
  58.8 86.1 %collective-permute-done.1 = bf16[512,2048]{1,0:T(8,128)(2,1)} collective-permute-done((bf16[512,2048]{1,0:T(8,128)(2,1)}, bf16[512,2048]{1,0:T(8,128)(2,1)}, u32[]{:S(2)}, u32[]{:S(2)}) %collective-permute-start.1) | collective-permute-done | bytes 2097184 | tf_op jit(solution)/shard_map/ppermute | solution.py:143
  144.8 5.2 fusion.100
  150.2 6.5 fusion.60
  157.1 7.5 fusion.8
  164.6 9.2 exponential_reduce_fusion
  179.6 6.3 convolution_convert_fusion.6
  186.0 4.3 convolution_convert_fusion.5
  190.5 6.4 convolution_convert_fusion.2
  196.9 3.9 copy.55
  202.9 71.1 %reduce-scatter.13.cloned.1.call-done = bf16[256,2048]{1,0:T(8,128)(2,1)} async-done(((bf16[1024,2048]{1,0:T(8,128)(2,1)}), bf16[256,2048]{1,0:T(8,128)(2,1)}) %reduce-scatter.13.cloned.1.call-update) | async-done | bytes 1048592 | tf_op jit(solution)/shard_map/reduce_scatter | solution.py:155
  278.9 23.1 %collective-permute-done.2 = bf16[256,2048]{1,0:T(8,128)(2,1)S(1)} collective-permute-done((bf16[256,2048]{1,0:T(8,128)(2,1)S(1)}, bf16[256,2048]{1,0:T(8,128)(2,1)S(1)}, u32[]{:S(2)}, u32[]{:S(2)}) %collective-permute-start.2) | collective-permute-done | bytes 1048608 | tf_op jit(solution)/shard_map/ppermute | solution.py:143
  306.2 60.3 %all-gather.24.cloned.1.call-done = bf16[1,2048,2,2048]{3,1,2,0:T(8,128)(2,1)} async-done(((bf16[1,256,2,2048]{3,1,2,0:T(8,128)(2,1)}), bf16[1,2048,2,2048]{3,1,2,0:T(8,128)(2,1)}) %all-gather.24.cloned.1.call-update) | async-done | bytes 16777232 | tf_op jit(solution)/shard_map/all_gather | solution.py:179
  366.6 22.6 %copy.56 = bf16[1,2048,2,2048]{1,3,2,0:T(8,128)(2,1)} copy(bf16[1,2048,2,2048]{3,1,2,0:T(8,128)(2,1)} %all-gather.24.cloned.1.call-done) | data formatting | bytes 33554432 | tf_op jit(solution)/shard_map/all_gather | solution.py:179
  389.1 51.2 %collective-permute-done.3 = bf16[512,2048]{1,0:T(8,128)(2,1)} collective-permute-done((bf16[512,2048]{1,0:T(8,128)(2,1)S(1)}, bf16[512,2048]{1,0:T(8,128)(2,1)}, u32[]{:S(2)}, u32[]{:S(2)}) %collective-permute-start.3) | collective-permute-done | bytes 2097184 | tf_op jit(solution)/shard_map/ppermute | solution.py:143
  440.3 24.6 %fusion = f32[1024,2,2048]{2,0,1:T(8,128)} fusion(bf16[1,2048,2,2048]{1,3,2,0:T(8,128)(2,1)} %copy.56, bf16[512,2048]{1,0:T(8,128)(2,1)} %collective-permute-done.3, bf16[512,2048]{1,0:T(8,128)(2,1)S(1)} %maximum_select_fusion.3, pred[]{:T(512)S(6)} %eq.46), kind=kOutput, calls=%fused_computation.1 | convolution fusion | flops 17198743552 | bytes 37748736 | tf_op jit(solution)/shard_map/dot_general | solution.py:217
  464.9 57.1 %all-gather.26.cloned.1.call-done = bf16[1,2048,2048]{2,1,0:T(8,128)(2,1)} async-done(((bf16[1,2048,256]{2,1,0:T(8,128)(2,1)}), bf16[1,2048,2048]{2,1,0:T(8,128)(2,1)}) %all-gather.26.cloned.1.call-update) | async-done | bytes 8388624 | tf_op jit(solution)/shard_map/all_gather | solution.py:180
  522.1 20.5 %multiply_bitcast_fusion.1 = (bf16[1024,1,2048]{2,0,1:T(8,128)(2,1)}, bf16[1024,1,2048]{2,0,1:T(8,128)(2,1)}) fusion(f32[1024,2,2048]{2,0,1:T(8,128)} %fusion, bf16[1024,2048]{1,0:T(8,128)(2,1)} %all-gather.14.cloned.1.call-done, bf16[1,2048,2048]{2,1,0:T(8,128)(2,1)} %all-gather.26.cloned.1.call-done), kind=kOutput, calls=%fused_computation.31 | convolution fusion | flops 8617197568 | bytes 37748736 | tf_op jit(solution)/shard_map/dot_general | solution.py:273
  542.5 24.2 %bitcast_convert_fusion = bf16[1024,2048]{1,0:T(8,128)(2,1)} fusion(bf16[1,2048,2,2048]{3,1,2,0:T(8,128)(2,1)} %all-gather.24.cloned.1.call-done, bf16[1024,1,2048]{2,0,1:T(8,128)(2,1)} %get-tuple-element.41, bf16[1024,1,2048]{2,0,1:T(8,128)(2,1)} %get-tuple-element.40), kind=kOutput, calls=%fused_computation.24 | convolution fusion | flops 17186160640 | bytes 29360128 | tf_op jit(solution)/shard_map/dot_general | solution.py:287
  566.9 76.9 %reduce-scatter.17.cloned.1.call-done = bf16[256,2048]{1,0:T(8,128)(2,1)} async-done(((bf16[1024,2048]{1,0:T(8,128)(2,1)}), bf16[256,2048]{1,0:T(8,128)(2,1)}) %reduce-scatter.17.cloned.1.call-update) | async-done | bytes 1048592 | tf_op jit(solution)/shard_map/reduce_scatter | solution.py:166
  649.2 81.3 %all-gather.16.cloned.1.call-done = bf16[1024,2048]{1,0:T(8,128)(2,1)} async-done(((bf16[256,2048]{1,0:T(8,128)(2,1)}), bf16[1024,2048]{1,0:T(8,128)(2,1)}) %all-gather.16.cloned.1.call-update) | async-done | bytes 4194320 | tf_op jit(solution)/shard_map/all_gather | solution.py:163
  730.6 5.2 fusion.63
  737.6 6.3 convolution_bitcast_fusion.4
  743.9 5.5 fusion.13
  753.4 9.3 fusion.4
  762.7 6.2 convolution_bitcast_fusion.1
  768.9 3.4 fusion.66
  772.3 6.5 fusion.67
  788.6 8.0 multiply_convert_fusion
  798.6 11.5 convolution_convert_fusion.1
  810.6 6.7 fusion.33
  817.4 5.8 convolution_convert_fusion.3
  823.3 7.2 convolution_convert_fusion.4
  830.6 13.9 %fusion.28 = bf16[1024,2048]{1,0:T(8,128)(2,1)} fusion(bf16[1024,2048]{1,0:T(8,128)(2,1)} %copy-done.14, bf16[1,2048,2048]{2,1,0:T(8,128)(2,1)} %all-gather.26.cloned.1.call-done), kind=kOutput, calls=%fused_computation.52 | convolution fusion | flops 8592031744 | bytes 16777216 | tf_op jit(solution)/shard_map/dot_general | solution.py:225
  844.6 7.6 maximum_convert_fusion
  852.2 11.9 copy.65
  867.8 24.1 %convolution_convert_fusion = bf16[2048,2,2048]{2,0,1:T(8,128)(2,1)} fusion(bf16[1024,2,2048]{0,2,1:T(8,128)(2,1)} %copy.65, bf16[512,2048]{1,0:T(8,128)(2,1)} %collective-permute-done.3, bf16[512,2048]{1,0:T(8,128)(2,1)S(1)} %copy-done.22, pred[]{:T(512)S(6)} %eq.46), kind=kOutput, calls=%fused_computation.14 | convolution fusion | flops 17207132160 | bytes 29360128 | tf_op jit(solution)/shard_map/dot_general | solution.py:282
  892.0 47.3 %reduce-scatter.29.cloned.1.call-done = bf16[2048,256]{1,0:T(8,128)(2,1)} async-done(((bf16[2048,2048]{1,0:T(8,128)(2,1)}), bf16[2048,256]{1,0:T(8,128)(2,1)}) %reduce-scatter.29.cloned.1.call-update) | async-done | bytes 1048592 | tf_op jit(solution)/shard_map/reduce_scatter | solution.py:364
  942.0 36.3 %reduce-scatter.23.cloned.1.call-done = bf16[256,2,128]{2,0,1:T(8,128)(2,1)} async-done(((bf16[2048,2,128]{2,0,1:T(8,128)(2,1)}), bf16[256,2,128]{2,0,1:T(8,128)(2,1)}) %reduce-scatter.23.cloned.1.call-update) | async-done | bytes 131088 | tf_op jit(solution)/shard_map/reduce_scatter | solution.py:355
  980.1 43.2 %reduce-scatter.25.cloned.1.call-done = bf16[512,256]{1,0:T(8,128)(2,1)} async-done(((bf16[512,2048]{1,0:T(8,128)(2,1)}), bf16[512,256]{1,0:T(8,128)(2,1)}) %reduce-scatter.25.cloned.1.call-update) | async-done | bytes 262160 | tf_op jit(solution)/shard_map/reduce_scatter | solution.py:358
  1025.0 43.1 %reduce-scatter.21.cloned.1.call-done = bf16[256,512]{1,0:T(8,128)(2,1)} async-done(((bf16[2048,512]{1,0:T(8,128)(2,1)}), bf16[256,512]{1,0:T(8,128)(2,1)}) %reduce-scatter.21.cloned.1.call-update) | async-done | bytes 262160 | tf_op jit(solution)/shard_map/reduce_scatter | solution.py:352
  1069.9 77.1 %reduce-scatter.15.cloned.1.call-done = bf16[256,2048]{1,0:T(8,128)(2,1)} async-done(((bf16[1024,2048]{1,0:T(8,128)(2,1)}), bf16[256,2048]{1,0:T(8,128)(2,1)}) %reduce-scatter.15.cloned.1.call-update) | async-done | bytes 1048592 | tf_op jit(solution)/shard_map/reduce_scatter | solution.py:155
  1147.1 6.0 fusion.45
  1153.1 34.1 %reduce-scatter.31.cloned.1.call-done = f32[256,2]{1,0:T(8,128)} async-done(((f32[2048,2]{1,0:T(8,128)}), f32[256,2]{1,0:T(8,128)}) %reduce-scatter.31.cloned.1.call-update) | async-done | bytes 2064
  1188.1 12.2 psum.8
  1200.4 106.4 %reduce-scatter.27.cloned.1.call-done = bf16[256,2,2048]{2,0,1:T(8,128)(2,1)} async-done(((bf16[2048,2,2048]{2,0,1:T(8,128)(2,1)}), bf16[256,2,2048]{2,0,1:T(8,128)(2,1)}) %reduce-scatter.27.cloned.1.call-update) | async-done | bytes 2097168 | tf_op jit(solution)/shard_map/reduce_scatter | solution.py:361
  1308.9 5.3 copy.68
  (210 shorter events, 72.9 us)
Async XLA Ops:
  7.2 47.2 %copy-start.35 = (s32[1,1024]{1,0:T(1,128)S(1)}, s32[1,1024]{1,0:T(1,128)}, u32[]{:S(2)}) copy-start(s32[1,1024]{1,0:T(1,128)} %param.11) | copy-start | bytes 12292
  7.2 49.9 %all-gather.18.cloned.1.call-start = ((), (), s32[]{:S(2)}) async-start(), calls=%async_computation.21 | async-start | bytes 1179648 | tf_op jit(solution)/shard_map/all_gather | solution.py:177
  8.8 141.4 %all-gather.20.cloned.1.call-start = ((), (), s32[]{:S(2)}) async-start(), calls=%async_computation.22 | async-start | bytes 2359296 | tf_op jit(solution)/shard_map/all_gather | solution.py:176
  9.6 180.9 %all-gather.22.cloned.1.call-start = ((), (), s32[]{:S(2)}) async-start(), calls=%async_computation.23 | async-start | bytes 2359296 | tf_op jit(solution)/shard_map/all_gather | solution.py:178
  21.7 37.1 %copy-start.39 = (f32[256]{0:T(256)}, f32[256]{0:T(256)S(1)}, u32[]{:S(2)}) copy-start(f32[256]{0:T(256)S(1)} %add_rsqrt_fusion.1) | copy-start | bytes 3076
  21.8 624.1 %copy-start.31 = (f32[1,1,2048]{2,1,0:T(1,128)}, f32[1,1,2048]{2,1,0:T(1,128)S(1)}, u32[]{:S(2)}) copy-start(f32[1,1,2048]{2,1,0:T(1,128)S(1)} %get-tuple-element.54) | copy-start | bytes 24580
  23.9 25.5 %collective-permute-start = (bf16[256,2048]{1,0:T(8,128)(2,1)S(1)}, bf16[256,2048]{1,0:T(8,128)(2,1)S(1)}, u32[]{:S(2)}, u32[]{:S(2)}) collective-permute-start(bf16[256,2048]{1,0:T(8,128)(2,1)S(1)} %fusion.41), channel_id=1, source_target_pairs={{0,1},{1,0},{2,3},{3,2},{4,5},{5,4},{6,7},{7,6},{8,9},{9,8},{10,11... | collective-permute-start | bytes 3145736 | tf_op jit(solution)/shard_map/ppermute | solution.py:143
  51.7 93.2 %collective-permute-start.1 = (bf16[512,2048]{1,0:T(8,128)(2,1)}, bf16[512,2048]{1,0:T(8,128)(2,1)}, u32[]{:S(2)}, u32[]{:S(2)}) collective-permute-start(bf16[512,2048]{1,0:T(8,128)(2,1)} %maximum_select_fusion.2), channel_id=1, source_target_pairs={{0,2},{1,3},{2,0},{3,1},{4,6},{5,7},{6,4},{7,5},{8,10},{9,11},{10,... | collective-permute-start | bytes 6291464 | tf_op jit(solution)/shard_map/ppermute | solution.py:143
  54.3 219.7 %reduce-scatter.13.cloned.1.call-start = ((), (), s32[]{:S(2)}) async-start(), calls=%async_computation.10 | async-start | bytes 5242880 | tf_op jit(solution)/shard_map/reduce_scatter | solution.py:155
  56.6 100.1 %copy-start.16 = (f32[1024,32]{0,1:T(8,128)}, f32[1024,32]{0,1:T(8,128)S(1)}, u32[]{:S(2)}) copy-start(f32[1024,32]{0,1:T(8,128)S(1)} %get-tuple-element.58) | copy-start | bytes 393220
  57.1 128.8 %copy-start.12 = (pred[512,1024]{0,1:T(8,128)(4,1)}, pred[512,1024]{0,1:T(8,128)(4,1)S(1)}, u32[]{:S(2)}) copy-start(pred[512,1024]{0,1:T(8,128)(4,1)S(1)} %fusion.62) | copy-start | bytes 1572868
  150.2 23.6 %copy-start.17 = (bf16[1024,2,32]{0,2,1:T(8,128)(2,1)}, bf16[1024,2,32]{0,2,1:T(8,128)(2,1)S(1)}, u32[]{:S(2)}) copy-start(bf16[1024,2,32]{0,2,1:T(8,128)(2,1)S(1)} %get-tuple-element.48) | copy-start | bytes 393220
  150.2 23.6 %copy-start.19 = (bf16[1024,2,32]{0,2,1:T(8,128)(2,1)}, bf16[1024,2,32]{0,2,1:T(8,128)(2,1)S(1)}, u32[]{:S(2)}) copy-start(bf16[1024,2,32]{0,2,1:T(8,128)(2,1)S(1)} %get-tuple-element.49) | copy-start | bytes 393220
  157.1 16.7 %copy-start.8 = (bf16[1024,2,4,32]{0,3,2,1:T(8,128)(2,1)}, bf16[1024,2,4,32]{0,3,2,1:T(8,128)(2,1)S(1)}, u32[]{:S(2)}) copy-start(bf16[1024,2,4,32]{0,3,2,1:T(8,128)(2,1)S(1)} %get-tuple-element.44) | copy-start | bytes 1572868
  157.1 16.7 %copy-start.10 = (bf16[1024,2,4,32]{0,3,2,1:T(8,128)(2,1)}, bf16[1024,2,4,32]{0,3,2,1:T(8,128)(2,1)S(1)}, u32[]{:S(2)}) copy-start(bf16[1024,2,4,32]{0,3,2,1:T(8,128)(2,1)S(1)} %get-tuple-element.45) | copy-start | bytes 1572868
  173.8 12.1 copy-start.38
  173.8 12.1 slice-start
  173.8 12.1 slice-start.1
  196.9 169.7 %all-gather.24.cloned.1.call-start = ((), (), s32[]{:S(2)}) async-start(), calls=%async_computation.24 | async-start | bytes 18874368 | tf_op jit(solution)/shard_map/all_gather | solution.py:179
  200.8 73.1 %copy-start = (bf16[256,2048]{1,0:T(8,128)(2,1)S(1)}, bf16[256,2048]{1,0:T(8,128)(2,1)}, u32[]{:S(2)}) copy-start(bf16[256,2048]{1,0:T(8,128)(2,1)} %param.10) | copy-start | bytes 3145732
  200.9 264.1 %all-gather.14.cloned.1.call-start = ((), (), s32[]{:S(2)}) async-start(), calls=%async_computation.12 | async-start | bytes 5242880 | tf_op jit(solution)/shard_map/all_gather | solution.py:163
  202.1 320.0 %all-gather.26.cloned.1.call-start = ((), (), s32[]{:S(2)}) async-start(), calls=%async_computation.25 | async-start | bytes 9437184 | tf_op jit(solution)/shard_map/all_gather | solution.py:180
  202.8 440.9 %reduce-scatter.17.cloned.1.call-start = ((), (), s32[]{:S(2)}) async-start(), calls=%async_computation.13 | async-start | bytes 5242880 | tf_op jit(solution)/shard_map/reduce_scatter | solution.py:166
  275.6 370.3 %copy-start.36 = (f32[256]{0:T(256)}, f32[256]{0:T(256)S(1)}, u32[]{:S(2)}) copy-start(f32[256]{0:T(256)S(1)} %add_rsqrt_fusion) | copy-start | bytes 3076
  277.3 24.6 %collective-permute-start.2 = (bf16[256,2048]{1,0:T(8,128)(2,1)S(1)}, bf16[256,2048]{1,0:T(8,128)(2,1)S(1)}, u32[]{:S(2)}, u32[]{:S(2)}) collective-permute-start(bf16[256,2048]{1,0:T(8,128)(2,1)S(1)} %multiply_convert_fusion.1), channel_id=1, source_target_pairs={{0,1},{1,0},{2,3},{3,2},{4,5},{5,4},{6,7},{7,6},{8,9},{9,8},{10,11... | collective-permute-start | bytes 3145736 | tf_op jit(solution)/shard_map/ppermute | solution.py:143
  303.0 137.4 %copy-start.21 = (bf16[512,2048]{1,0:T(8,128)(2,1)}, bf16[512,2048]{1,0:T(8,128)(2,1)S(1)}, u32[]{:S(2)}) copy-start(bf16[512,2048]{1,0:T(8,128)(2,1)S(1)} %maximum_select_fusion.3) | copy-start | bytes 6291460
  303.0 137.3 %collective-permute-start.3 = (bf16[512,2048]{1,0:T(8,128)(2,1)S(1)}, bf16[512,2048]{1,0:T(8,128)(2,1)}, u32[]{:S(2)}, u32[]{:S(2)}) collective-permute-start(bf16[512,2048]{1,0:T(8,128)(2,1)S(1)} %maximum_select_fusion.3), channel_id=1, source_target_pairs={{0,2},{1,3},{2,0},{3,1},{4,6},{5,7},{6,4},{7,5},{8,10},{9,11},{10,... | collective-permute-start | bytes 6291464 | tf_op jit(solution)/shard_map/ppermute | solution.py:143
  566.8 77.0 %copy-start.2 = (bf16[256,2048]{1,0:T(8,128)(2,1)S(1)}, bf16[256,2048]{1,0:T(8,128)(2,1)}, u32[]{:S(2)}) copy-start(bf16[256,2048]{1,0:T(8,128)(2,1)} %reduce-scatter.13.cloned.1.call-done) | copy-start | bytes 3145732
  566.8 163.8 %all-gather.16.cloned.1.call-start = ((), (), s32[]{:S(2)}) async-start(), calls=%async_computation.14 | async-start | bytes 5242880 | tf_op jit(solution)/shard_map/all_gather | solution.py:163
  645.9 84.7 %copy-start.41 = (f32[256]{0:T(256)}, f32[256]{0:T(256)S(1)}, u32[]{:S(2)}) copy-start(f32[256]{0:T(256)S(1)} %broadcast_multiply_fusion.2) | copy-start | bytes 3076
  649.2 86.6 %copy-start.24 = (bf16[2,64,4,512]{3,1,2,0:T(8,128)(2,1)S(1)}, bf16[2,64,4,512]{3,1,2,0:T(8,128)(2,1)}, u32[]{:S(2)}) copy-start(bf16[2,64,4,512]{3,1,2,0:T(8,128)(2,1)} %copy-done.23) | copy-start | bytes 1572868
  649.2 86.6 %copy-start.26 = (bf16[2,64,4,512]{3,1,2,0:T(8,128)(2,1)S(1)}, bf16[2,64,4,512]{3,1,2,0:T(8,128)(2,1)}, u32[]{:S(2)}) copy-start(bf16[2,64,4,512]{3,1,2,0:T(8,128)(2,1)} %copy-done.25) | copy-start | bytes 1572868
  649.2 214.9 %reduce-scatter.19.cloned.1.call-start = ((), (), s32[]{:S(2)}) async-start(), calls=%async_computation.15 | async-start | bytes 5242880 | tf_op jit(solution)/shard_map/reduce_scatter | solution.py:166
  737.5 15.8 %slice-start.4 = ((s8[16777216]{0:T(1024)(128)(4,1)}), s8[4194304]{0:T(1024)(128)(4,1)S(1)}, s32[]{:S(2)}) async-start(s8[16777216]{0:T(1024)(128)(4,1)} %bitcast.274), calls=%async_computation.31 | async-start | bytes 8388608
  737.6 15.8 %slice-start.5 = ((s8[16777216]{0:T(1024)(128)(4,1)}), s8[4194304]{0:T(1024)(128)(4,1)S(1)}, s32[]{:S(2)}) async-start(s8[16777216]{0:T(1024)(128)(4,1)} %bitcast.274), calls=%async_computation.32 | async-start | bytes 8388608
  788.5 150.7 %reduce-scatter.29.cloned.1.call-start = ((), (), s32[]{:S(2)}) async-start(), calls=%async_computation.20 | async-start | bytes 9437184 | tf_op jit(solution)/shard_map/reduce_scatter | solution.py:364
  810.1 168.2 %reduce-scatter.23.cloned.1.call-start = ((), (), s32[]{:S(2)}) async-start(), calls=%async_computation.17 | async-start | bytes 1179648 | tf_op jit(solution)/shard_map/reduce_scatter | solution.py:355
  817.3 206.0 %reduce-scatter.25.cloned.1.call-start = ((), (), s32[]{:S(2)}) async-start(), calls=%async_computation.18 | async-start | bytes 2359296 | tf_op jit(solution)/shard_map/reduce_scatter | solution.py:358
  823.2 244.9 %reduce-scatter.21.cloned.1.call-start = ((), (), s32[]{:S(2)}) async-start(), calls=%async_computation.16 | async-start | bytes 2359296 | tf_op jit(solution)/shard_map/reduce_scatter | solution.py:352
  830.5 316.5 %reduce-scatter.15.cloned.1.call-start = ((), (), s32[]{:S(2)}) async-start(), calls=%async_computation.11 | async-start | bytes 5242880 | tf_op jit(solution)/shard_map/reduce_scatter | solution.py:155
  844.5 342.7 %reduce-scatter.31.cloned.1.call-start = ((), (), s32[]{:S(2)}) async-start(), calls=%async_computation.26 | async-start | bytes 1179648
  852.2 11.9 copy-start.40
  867.5 439.3 %reduce-scatter.27.cloned.1.call-start = ((), (), s32[]{:S(2)}) async-start(), calls=%async_computation.19 | async-start | bytes 18874368 | tf_op jit(solution)/shard_map/reduce_scatter | solution.py:361
  891.9 255.1 %copy-start.3 = (bf16[256,2048]{1,0:T(8,128)(2,1)S(1)}, bf16[256,2048]{1,0:T(8,128)(2,1)}, u32[]{:S(2)}) copy-start(bf16[256,2048]{1,0:T(8,128)(2,1)} %reduce-scatter.13.cloned.1.call-done) | copy-start | bytes 3145732
  891.9 255.1 %copy-start.6 = (bf16[256,2048]{1,0:T(8,128)(2,1)S(1)}, bf16[256,2048]{1,0:T(8,128)(2,1)}, u32[]{:S(2)}) copy-start(bf16[256,2048]{1,0:T(8,128)(2,1)} %reduce-scatter.17.cloned.1.call-done) | copy-start | bytes 3145732
  892.0 255.1 %copy-start.32 = (f32[1,1,2048]{2,1,0:T(1,128)S(1)}, f32[1,1,2048]{2,1,0:T(1,128)}, u32[]{:S(2)}) copy-start(f32[1,1,2048]{2,1,0:T(1,128)} %copy-done.31) | copy-start | bytes 24580
  892.0 255.1 %copy-start.37 = (f32[256]{0:T(256)S(1)}, f32[256]{0:T(256)}, u32[]{:S(2)}) copy-start(f32[256]{0:T(256)} %copy-done.36) | copy-start | bytes 3076
  892.0 255.1 %copy-start.42 = (f32[256]{0:T(256)S(1)}, f32[256]{0:T(256)}, u32[]{:S(2)}) copy-start(f32[256]{0:T(256)} %copy-done.41) | copy-start | bytes 3076
  (27 other events, 138.3 us)
Sparse Core Ops, SparseCore 0:
  10.5 26.0 all-gather.17
  38.5 27.7 all-gather.19
  68.2 28.0 all-gather.21
  197.0 76.9 reduce-scatter.12
  276.3 90.2 all-gather.23
  368.5 95.6 all-gather.13
  466.1 55.8 all-gather.25
  566.9 76.7 reduce-scatter.16
  649.3 81.2 all-gather.15
  788.6 75.2 reduce-scatter.18
  867.4 71.7 reduce-scatter.28
  942.3 35.9 reduce-scatter.22
  982.1 41.1 reduce-scatter.24
  1027.0 41.0 reduce-scatter.20
  1070.2 76.7 reduce-scatter.14
  1150.7 36.4 reduce-scatter.30
  1190.6 116.1 reduce-scatter.26
